TPU v7x, 32 devices: a whole 2x2x4 slice. The times are simulated.
32 devices in a mesh: node: 4 (over z), local: 8 (over y, x, core).
Axes of the slice: x: 2, y: 2, z: 4, core: 2. Of those that a mesh axis runs over, the one named last changes fastest.
Arguments:
- tokens: bfloat16 [4096, 5120], P(('node', 'local')), may hold values from -6 to 6
- routes: int32 [4096, 6], P(('node', 'local')), may hold values from 0 to 31, all different within a row; in each aligned block of 128 rows (0 to 127, 128 to 255, ...) at most 32 rows name the same one
- route_weights: float32 [4096, 6], P(('node', 'local')), may hold values from 0.05 to 1
- w_gate: bfloat16 [32, 5120, 768], P(('node', 'local')), may hold values from -0.078125 to 0.078125
- w_up: bfloat16 [32, 5120, 768], P(('node', 'local')), may hold values from -0.078125 to 0.078125
- w_down: bfloat16 [32, 768, 5120], P(('node', 'local')), may hold values from -0.21875 to 0.21875
Outputs:
- mixed: bfloat16 [4096, 5120], P(('node', 'local'))
- balance_loss: float32 [], replicated
Inputs may be any that keep to these rules, and one draw needn't show every extreme that they name: `routes`: each row names 6 different experts. Among the rows of one device no expert is named more than 32 times, a bound that some block reaches.
All inputs are finite; a program needn't handle non-finite values.
Results may differ from a plain program's by a relative error of at most 0.0025.
The roundings to bfloat16 on the way count: a program that leaves them out, or rounds other values in their place, can miss the bound.
Values may be sent and summed in bfloat16 or wider, within the bound.
A program may use at most 128 MiB of HBM per device.

v0:
```python
import jax
import jax.numpy as jnp
from jax import lax
from jax.sharding import PartitionSpec as P

TOPK = 6


def expert_apply(rows, w_gate, w_up, w_down):
    gate = jnp.einsum("erd,edf->erf", rows, w_gate, preferred_element_type=jnp.float32)
    upper = jnp.einsum("erd,edf->erf", rows, w_up, preferred_element_type=jnp.float32)
    hidden = (jax.nn.silu(gate) * upper).astype(jnp.bfloat16)
    return jnp.einsum("erf,efd->erd", hidden, w_down, preferred_element_type=jnp.float32).astype(
        jnp.bfloat16
    )


def local(tokens, routes, route_weights, w_gate, w_up, w_down):
    n_node = lax.axis_size("node")
    n_local = lax.axis_size("local")
    exp_dev = w_gate.shape[0]
    devices = n_node * n_local
    experts = exp_dev * devices
    tok_dev = tokens.shape[0]
    width = tokens.shape[1]
    capacity = 4 * tok_dev * TOPK // (3 * experts)
    flat = routes.reshape(-1)
    labels = jnp.arange(experts, dtype=jnp.int32)
    onehot = (flat[:, None] == labels[None, :]).astype(jnp.int32)
    running = jnp.cumsum(onehot, axis=0) - onehot
    slots = jnp.sum(running * onehot, axis=1)
    position = flat * capacity + slots
    counts = jnp.sum(onehot, axis=0).astype(jnp.float32)
    weight_sums = jnp.sum(onehot.astype(jnp.float32) * route_weights.reshape(-1)[:, None], axis=0)
    counts_all, sums_all = lax.psum((counts, weight_sums), ("node", "local"))
    repeated = jnp.repeat(tokens, TOPK, axis=0)
    outgoing = jnp.zeros((experts * capacity, width), jnp.bfloat16).at[position].set(repeated)
    piece = lax.all_to_all(
        outgoing.reshape(experts, 1, capacity, width),
        ("node", "local"),
        split_axis=0,
        concat_axis=1,
        tiled=True,
    )
    held, sources, count, breadth = piece.shape
    rows = piece.reshape(held, sources * count, breadth)
    result = expert_apply(rows, w_gate, w_up, w_down)
    result = result.reshape(held, sources, count, breadth)
    returned = lax.all_to_all(result, ("node", "local"), split_axis=1, concat_axis=0, tiled=True)
    returned = returned.reshape(experts * capacity, width)
    picked = returned[position].reshape(tok_dev, TOPK, width).astype(jnp.float32)
    mixed = jnp.sum(route_weights[:, :, None] * picked, axis=1).astype(jnp.bfloat16)
    total = jnp.float32(tok_dev * devices)
    balance_loss = (
        jnp.sum(counts_all * sums_all) * jnp.float32(experts) / (jnp.float32(TOPK) * total * total)
    )
    return (mixed, balance_loss)


def solution(mesh):
    placed = (
        P(("node", "local"), None),
        P(("node", "local"), None),
        P(("node", "local"), None),
        P(("node", "local"), None, None),
        P(("node", "local"), None, None),
        P(("node", "local"), None, None),
    )
    return jax.shard_map(
        local,
        mesh=mesh,
        in_specs=placed,
        out_specs=(P(("node", "local"), None), P()),
        check_vma=False,
    )
```

profile of v0, /device:TPU:27, one launch (start us, length us, event | category | flops | bytes accessed | tf_op | source)
XLA Modules:
  0.0 614.8 jit_solution(2982418131425307916)
XLA Ops:
  0.6 0.8 copy.17
  1.4 0.1 eq.29
  1.6 0.1 eq.25
  1.7 0.7 broadcast_multiply_fusion
  2.4 1.7 reduce-window.6
  4.1 0.3 slice_reduce_fusion
  4.5 0.1 mul.53
  4.7 6.3 %broadcast_in_dim.5 = bf16[128,6,5120]{2,1,0:T(8,128)(2,1)} broadcast(bf16[128,5120]{1,0:T(8,128)(2,1)} %param.6), dimensions={0,2} | broadcast | bytes 9175040 | tf_op jit(solution)/shard_map/broadcast_in_dim | solution.py:36
  11.0 13.2 %reshape.127 = bf16[768,5120]{1,0:T(8,128)(2,1)} reshape(bf16[128,6,5120]{2,1,0:T(8,128)(2,1)} %broadcast_in_dim.5) | data formatting | bytes 15728640 | tf_op jit(solution)/shard_map/reshape | solution.py:36
  24.2 0.1 convert_reduce_fusion
  24.4 21.7 %scatter_custom_fusion = bf16[1024,5120]{1,0:T(8,128)(2,1)} fusion(s32[768]{0:T(1024)S(1)} %fusion.14, bf16[768,5120]{1,0:T(8,128)(2,1)} %reshape.127, bf16[]{:T(256)} %constant.7.clone.1), kind=kCustom, calls=%fused_computation.9 | custom fusion | bytes 10486272 | tf_op jit(solution)/shard_map/scatter | solution.py:37
  46.1 231.7 %all_to_all.8 = bf16[32,1,32,5120]{3,2,1,0:T(8,128)(2,1)S(1)} all-to-all(bf16[32,1,32,5120]{3,2,1,0:T(8,128)(2,1)} %bitcast.32), channel_id=1, replica_groups=mesh['node'=4,'local'=8] {'node','local'}, dimensions={0} | all-to-all | bytes 20971520 | tf_op jit(solution)/shard_map/all_to_all | solution.py:38
  277.8 10.9 %fusion.1 = f32[1024,768]{1,0:T(8,128)S(1)} fusion(bf16[1024,5120]{1,0:T(8,128)(2,1)S(1)} %bitcast.34, bf16[1,5120,768]{2,1,0:T(8,128)(2,1)} %param.10), kind=kOutput, calls=%fused_computation.5 | convolution fusion | flops 8053063680 | bytes 21495808 | tf_op jit(solution)/shard_map/erd,edf->erf/dot_general | solution.py:11
  288.7 8.6 %multiply_convert_fusion = bf16[1024,768]{1,0:T(8,128)(2,1)S(1)} fusion(f32[1024,768]{1,0:T(8,128)S(1)} %fusion.1, bf16[1024,5120]{1,0:T(8,128)(2,1)S(1)} %bitcast.35, bf16[1,5120,768]{2,1,0:T(8,128)(2,1)S(1)} %bitcast.38), kind=kOutput, calls=%fused_computation.11 | convolution fusion | flops 8057782272 | bytes 23068672 | tf_op jit(solution)/shard_map/erd,edf->erf/dot_general | solution.py:10
  297.3 13.7 %convolution_convert_fusion = bf16[1024,5120]{1,0:T(8,128)(2,1)} fusion(bf16[1024,768]{1,0:T(8,128)(2,1)S(1)} %multiply_convert_fusion, bf16[1,768,5120]{2,1,0:T(8,128)(2,1)} %param.11), kind=kOutput, calls=%fused_computation.3 | convolution fusion | flops 8058306560 | bytes 19922944 | tf_op jit(solution)/shard_map/erf,efd->erd/dot_general | solution.py:13
  311.0 6.7 %all-to-all-start.1 = ((bf16[1,32,32,5120]{3,2,0,1:T(8,128)(2,1)}), bf16[1,32,32,5120]{3,2,0,1:T(8,128)(2,1)}, u32[]{:S(2)}, u32[]{:S(2)}) async-start(bf16[1,32,32,5120]{3,2,0,1:T(8,128)(2,1)} %bitcast.33), calls=%async_computation.1 | async-start | bytes 20971520 | tf_op jit(solution)/shard_map/all_to_all | solution.py:49
  317.8 0.1 copy.15
  317.9 0.1 mul.58
  318.0 0.1 fusion.12
  318.2 247.9 %all-reduce = (f32[32]{0:T(128)S(1)}, f32[32]{0:T(128)S(1)}) all-reduce(f32[32]{0:T(128)S(1)} %convert_element_type.37, f32[32]{0:T(128)S(1)} %fusion.12), channel_id=1, replica_groups=mesh['node'=4,'local'=8] {'node','local'}, use_global_device_ids=true, to_apply=%region_6.7 | all-reduce | flops 64 | bytes 512 | tf_op jit(solution)/shard_map/psum | solution.py:35
  566.1 0.6 multiply_reduce_fusion.1
  567.4 20.0 %gather_fusion = bf16[768,5120]{1,0:T(8,128)(2,1)} fusion(bf16[1024,5120]{1,0:T(8,128)(2,1)} %bitcast.8, s32[1024]{0:T(1024)S(1)} %pad_clamp_fusion), kind=kCustom, calls=%fused_computation | custom fusion | bytes 15731712 | tf_op jit(solution)/shard_map/gather | solution.py:51
  587.4 14.3 %reshape.114 = f32[128,6,5120]{2,1,0:T(8,128)} reshape(bf16[768,5120]{1,0:T(8,128)(2,1)} %gather_fusion) | data formatting | bytes 23592960 | tf_op jit(solution)/shard_map/convert_element_type | solution.py:51
  601.7 12.0 %multiply_reduce_fusion = bf16[128,5120]{1,0:T(8,128)(2,1)} fusion(f32[128,6,5120]{2,1,0:T(8,128)} %reshape.114, f32[128,6]{1,0:T(8,128)S(1)} %copy.15), kind=kLoop, calls=%fused_computation.2 | loop fusion | flops 7208960 | bytes 17042432 | tf_op jit(solution)/shard_map/reduce_sum | solution.py:52
  (14 shorter events, 0.2 us)
Async XLA Ops:
  46.1 242.6 %slice-start = ((s8[7864320]{0:T(1024)(128)(4,1)}), s8[4194304]{0:T(1024)(128)(4,1)S(1)}, s32[]{:S(2)}) async-start(s8[7864320]{0:T(1024)(128)(4,1)} %bitcast.37), calls=%async_computation.2 | async-start | bytes 8388608
  277.8 10.9 %slice-start.1 = ((s8[7864320]{0:T(1024)(128)(4,1)}), s8[3670016]{0:T(1024)(128)(4,1)S(1)}, s32[]{:S(2)}) async-start(s8[7864320]{0:T(1024)(128)(4,1)} %bitcast.37), calls=%async_computation.3 | async-start | bytes 7340032
  311.0 6.7 %copy-start = (f32[128,6]{0,1:T(8,128)S(1)}, f32[128,6]{0,1:T(8,128)}, u32[]{:S(2)}) copy-start(f32[128,6]{0,1:T(8,128)} %param.8) | copy-start | bytes 9220
  311.0 256.3 %all-to-all-start.1 = ((bf16[1,32,32,5120]{3,2,0,1:T(8,128)(2,1)}), bf16[1,32,32,5120]{3,2,0,1:T(8,128)(2,1)}, u32[]{:S(2)}, u32[]{:S(2)}) async-start(bf16[1,32,32,5120]{3,2,0,1:T(8,128)(2,1)} %bitcast.33), calls=%async_computation.1 | async-start | bytes 20971520 | tf_op jit(solution)/shard_map/all_to_all | solution.py:49
where the time goes:
time: 620 us; the launch traced here: 615 us
  blocking collectives  480 us (77%)
  local copies, waits for them, and re-layouts  77.4 us (12%)
  matrix products  33.2 us (5%)
  other arithmetic  15.4 us (2%)
  starting transfers between devices  6.72 us (1%)
    psum x1, blocking collectives, local(): counts_all, sums_all = lax.psum((counts, weight_sums), ('node', 'local'))  248 us
    all_to_all x1, blocking collectives, local(): lax.all_to_all(outgoing.reshape(experts, 1, capacity, width), ('node', 'l...  232 us
    scatter x1, local copies, waits for them, and re-layouts, local(): jnp.zeros((experts * capacity, width), jnp.bfloat16).at[position]  21.7 us
    gather x1, local copies, waits for them, and re-layouts, local(): returned[position].reshape(tok_dev, TOPK, width).astype(jnp.float32)  20 us
    convert_element_type x1, local copies, waits for them, and re-layouts, local(): returned[position].reshape(tok_dev, TOPK, width).astype(jnp.float32)  14.3 us
    dot_general x1, matrix products, expert_apply(): jnp.einsum('erf,efd->erd', hidden, w_down, preferred_element_type=jnp.flo...  13.7 us
    reshape x1, local copies, waits for them, and re-layouts, local(): repeated = jnp.repeat(tokens, TOPK, axis=0)  13.2 us
  transfers between devices with their start and end apart: 1, of which 0 were waited for; matrix products, arithmetic and copies ran while one was open for 0% of the time, Pallas kernels for 0%

commit v1 on v0

v1 whole, which is shorter than its diff:
```python
import functools

import jax
import jax.numpy as jnp
from jax import lax
from jax.experimental import pallas as pl
from jax.experimental.pallas import tpu as pltpu
from jax.sharding import PartitionSpec as P

MESH = pl.DeviceIdType.MESH
VMEM_LIMIT = 62 * 1024 * 1024


def chunks_of(width):
    return max(n for n in range(1, 9) if width % (n * 128) == 0)


def greet(nn, nl, mn, ml):
    barrier = pltpu.get_barrier_semaphore()
    for k in range(1, nn):
        pl.semaphore_signal(barrier, inc=1, device_id={"node": lax.rem(mn + k, nn)}, device_id_type=MESH)
    for k in range(1, nl):
        pl.semaphore_signal(barrier, inc=1, device_id={"local": lax.rem(ml + k, nl)}, device_id_type=MESH)
    pl.semaphore_wait(barrier, nn + nl - 2)


def dispatch_kernel(nn, nl, nch, tok, pick, out, held, sent, z_send, z_recv, p_send, p_recv, own_sem):
    mn, ml = lax.axis_index("node"), lax.axis_index("local")
    tok_dev, width = tok.shape
    ch = width // nch
    rows = out.shape[1]
    mine = pl.ds(pl.multiple_of(mn * tok_dev, tok_dev), tok_dev)

    def cols(c):
        return pl.ds(pl.multiple_of(c * ch, 128), ch)

    def along(c, k):
        return pltpu.make_async_remote_copy(
            src_ref=tok.at[:, cols(c)],
            dst_ref=held.at[c, mine, :],
            send_sem=z_send.at[c, k - 1],
            recv_sem=z_recv.at[c, k - 1],
            device_id={"node": lax.rem(mn + k, nn)},
            device_id_type=MESH,
        )

    def block(e):
        return pl.ds(pl.multiple_of(e * rows, rows), rows)

    def within(c, k):
        e = lax.rem(ml + k, nl)
        return pltpu.make_async_remote_copy(
            src_ref=sent.at[c, block(e), :],
            dst_ref=out.at[ml, :, cols(c)],
            send_sem=p_send.at[c, k - 1],
            recv_sem=p_recv.at[c, k - 1],
            device_id={"local": e},
            device_id_type=MESH,
        )

    def own(c):
        return pltpu.make_async_copy(sent.at[c, block(ml), :], out.at[ml, :, cols(c)], own_sem.at[c])

    greet(nn, nl, mn, ml)

    @pl.loop(0, nch)
    def _(c):
        for k in range(1, nn):
            along(c, k).start()

    @pl.loop(0, nch)
    def _(c):
        held[c, mine, :] = tok[:, cols(c)]

    @pl.loop(0, nch)
    def _(c):
        for k in range(1, nn):
            along(c, k).wait_recv()
        picked = jnp.dot(pick[...], held[c], preferred_element_type=jnp.float32)
        sent[c] = picked.astype(jnp.bfloat16)
        for k in range(1, nl):
            within(c, k).start()
        own(c).start()

    @pl.loop(0, nch)
    def _(c):
        for k in range(1, nl):
            within(c, k).wait_recv()
        own(c).wait()
        for k in range(1, nn):
            along(c, k).wait_send()
        for k in range(1, nl):
            within(c, k).wait_send()


def return_kernel(nn, nl, nch, y, mix, out, held, part, got, p_send, p_recv, z_send, z_recv, own_sem):
    mn, ml = lax.axis_index("node"), lax.axis_index("local")
    tok_dev, width = out.shape
    ch = width // nch
    rows = y.shape[1]
    lines = nn * tok_dev
    mine = pl.ds(pl.multiple_of(ml * rows, rows), rows)

    def cols(c):
        return pl.ds(pl.multiple_of(c * ch, 128), ch)

    def within(c, k):
        e = lax.rem(ml + k, nl)
        return pltpu.make_async_remote_copy(
            src_ref=y.at[e, :, cols(c)],
            dst_ref=held.at[c, mine, :],
            send_sem=p_send.at[c, k - 1],
            recv_sem=p_recv.at[c, k - 1],
            device_id={"local": e},
            device_id_type=MESH,
        )

    def own(c):
        return pltpu.make_async_copy(y.at[ml, :, cols(c)], held.at[c, mine, :], own_sem.at[c])

    def tokens_of(p):
        return pl.ds(pl.multiple_of(p * tok_dev, tok_dev), tok_dev)

    def along(c, k):
        p = lax.rem(mn + k, nn)
        return pltpu.make_async_remote_copy(
            src_ref=part.at[c, tokens_of(p), :],
            dst_ref=got.at[c, k - 1],
            send_sem=z_send.at[c, k - 1],
            recv_sem=z_recv.at[c, k - 1],
            device_id={"node": p},
            device_id_type=MESH,
        )

    greet(nn, nl, mn, ml)

    @pl.loop(0, nch)
    def _(c):
        for k in range(1, nl):
            within(c, k).start()
        own(c).start()

    @pl.loop(0, nch)
    def _(c):
        for k in range(1, nl):
            within(c, k).wait_recv()
        own(c).wait()
        terms = [
            jnp.dot(mix[pl.ds(i * lines, lines), :], held[c], preferred_element_type=jnp.float32)
            for i in range(3)
        ]
        part[c] = terms[0] + terms[1] + terms[2]
        for k in range(1, nn):
            along(c, k).start()

    @pl.loop(0, nch)
    def _(c):
        total = part[c, tokens_of(mn), :]
        for k in range(1, nn):
            along(c, k).wait_recv()
        for k in range(1, nn):
            total = total + got[c, k - 1]
        out[:, cols(c)] = total.astype(out.dtype)
        for k in range(1, nl):
            within(c, k).wait_send()
        for k in range(1, nn):
            along(c, k).wait_send()


def sems(*shape):
    return pltpu.SemaphoreType.DMA(shape)


def local(tokens, routes, route_weights, w_gate, w_up, w_down):
    nn, nl = lax.axis_size("node"), lax.axis_size("local")
    mn, ml = lax.axis_index("node"), lax.axis_index("local")
    devices = nn * nl
    exp_dev = w_gate.shape[0]
    experts = exp_dev * devices
    assert exp_dev == 1
    tok_dev, width = tokens.shape
    topk = routes.shape[1]
    cap = 4 * tok_dev * topk // (3 * experts)
    rows = nn * cap
    nch = chunks_of(width)
    ch = width // nch
    f32, bf16 = jnp.float32, jnp.bfloat16

    both = jnp.concatenate([routes.astype(f32), route_weights], axis=1)
    every = lax.all_gather(both, ("node", "local"), axis=0, tiled=True)
    every_routes = every[:, :topk].astype(jnp.int32)
    labels = jnp.arange(experts, dtype=jnp.int32)
    hit = every_routes[:, :, None] == labels[None, None, :]
    counts = jnp.sum(hit.astype(f32), axis=(0, 1))
    sums = jnp.sum(jnp.where(hit, every[:, topk:, None], 0.0), axis=(0, 1))
    total = jnp.float32(tok_dev * devices)
    balance_loss = jnp.sum(counts * sums) * jnp.float32(experts) / (jnp.float32(topk) * total * total)

    line = lax.dynamic_index_in_dim(every.reshape(nn, nl, tok_dev, 2 * topk), ml, 1, keepdims=False)
    plane = mn * nl + jnp.arange(nl, dtype=jnp.int32)
    chosen = line[..., :topk, None].astype(jnp.int32) == plane
    named = jnp.any(chosen, axis=2)
    weight = jnp.sum(jnp.where(chosen, line[..., topk:, None], 0.0), axis=2)
    before = jnp.tril(jnp.ones((tok_dev, tok_dev), bf16), -1)
    slot = jnp.einsum("ut,pte->pue", before, named.astype(bf16), preferred_element_type=f32)
    slot = jnp.where(named, slot.astype(jnp.int32), -1)
    where = (
        (slot.transpose(2, 0, 1)[:, None, None] == jnp.arange(cap)[None, None, :, None, None])
        & (jnp.arange(nn)[:, None] == jnp.arange(nn)[None, :])[None, :, None, :, None]
    )
    pick = where.astype(bf16).reshape(nl * rows, nn * tok_dev)
    back = (
        (slot[:, :, :, None, None] == jnp.arange(cap)[None, None, None, None, :])
        & (jnp.arange(nn)[:, None] == jnp.arange(nn)[None, :])[:, None, None, :, None]
    )
    high = lax.reduce_precision(weight, 8, 7)
    middle = lax.reduce_precision(weight - high, 8, 7)
    low = lax.reduce_precision(weight - high - middle, 8, 7)
    mix = jnp.where(back[None], jnp.stack([high, middle, low])[..., None, None], 0.0).astype(bf16)
    mix = mix.reshape(3 * nn * tok_dev, nl * rows)

    vmem = pl.BlockSpec(memory_space=pltpu.VMEM)
    hbm = pl.BlockSpec(memory_space=pl.ANY)
    got = pl.pallas_call(
        functools.partial(dispatch_kernel, nn, nl, nch),
        out_shape=jax.ShapeDtypeStruct((nl, rows, width), bf16),
        in_specs=[vmem, vmem],
        out_specs=hbm,
        scratch_shapes=[
            pltpu.VMEM((nch, nn * tok_dev, ch), bf16),
            pltpu.VMEM((nch, nl * rows, ch), bf16),
            sems(nch, nn - 1),
            sems(nch, nn - 1),
            sems(nch, nl - 1),
            sems(nch, nl - 1),
            sems(nch),
        ],
        compiler_params=pltpu.CompilerParams(
            collective_id=0, has_side_effects=True, vmem_limit_bytes=VMEM_LIMIT
        ),
    )(tokens, pick)
    got = got.reshape(nl * rows, width)
    gate = jnp.dot(got, w_gate[0], preferred_element_type=f32)
    upper = jnp.dot(got, w_up[0], preferred_element_type=f32)
    hidden = (jax.nn.silu(gate) * upper).astype(bf16)
    y = jnp.dot(hidden, w_down[0], preferred_element_type=f32).astype(bf16)

    mixed = pl.pallas_call(
        functools.partial(return_kernel, nn, nl, nch),
        out_shape=jax.ShapeDtypeStruct((tok_dev, width), bf16),
        in_specs=[hbm, vmem],
        out_specs=vmem,
        scratch_shapes=[
            pltpu.VMEM((nch, nl * rows, ch), bf16),
            pltpu.VMEM((nch, nn * tok_dev, ch), f32),
            pltpu.VMEM((nch, nn - 1, tok_dev, ch), f32),
            sems(nch, nl - 1),
            sems(nch, nl - 1),
            sems(nch, nn - 1),
            sems(nch, nn - 1),
            sems(nch),
        ],
        compiler_params=pltpu.CompilerParams(
            collective_id=1, has_side_effects=True, vmem_limit_bytes=VMEM_LIMIT
        ),
    )(y.reshape(nl, rows, width), mix)
    return (mixed, balance_loss)


def solution(mesh):
    placed = (
        P(("node", "local"), None),
        P(("node", "local"), None),
        P(("node", "local"), None),
        P(("node", "local"), None, None),
        P(("node", "local"), None, None),
        P(("node", "local"), None, None),
    )
    return jax.shard_map(
        local,
        mesh=mesh,
        in_specs=placed,
        out_specs=(P(("node", "local"), None), P()),
        check_vma=False,
    )
```

time: 620 us -> 510 us (0.82)
  blocking collectives: 480 us -> 34.1 us
  Pallas kernels: 0 us -> 420 us
  local copies, waits for them, and re-layouts: 77.4 us -> 11.5 us
  other arithmetic: 15.4 us -> 7.54 us
  starting transfers between devices: 6.72 us -> 0 us
    pallas_call x0 -> x2, Pallas kernels: none -> 420 us  [the longest x1 260 us: local(): pl.pallas_call(functools.partial(return_kernel, nn, nl, nch), out_shape=j...]
    psum x1 -> x0, blocking collectives: 248 us -> none  [local(): counts_all, sums_all = lax.psum((counts, weight_sums), ('node', 'local'))]
    all_to_all x1 -> x0, blocking collectives: 232 us -> none  [local(): lax.all_to_all(outgoing.reshape(experts, 1, capacity, width), ('node', 'l...]
    all_gather x0 -> x1, blocking collectives: none -> 34.1 us  [local(): every = lax.all_gather(both, ('node', 'local'), axis=0, tiled=True)]
    scatter x1 -> x0, local copies, waits for them, and re-layouts: 21.7 us -> none  [local(): jnp.zeros((experts * capacity, width), jnp.bfloat16).at[position]]
    gather x1 -> x0, local copies, waits for them, and re-layouts: 20 us -> none  [local(): returned[position].reshape(tok_dev, TOPK, width).astype(jnp.float32)]
    reshape x1, local copies, waits for them, and re-layouts: 13.2 us -> 0.01 us  [local(): every.reshape(nn, nl, tok_dev, 2 * topk)]
    reduce_sum x4 -> x3, other arithmetic: 12.9 us -> 1.92 us  [the longest x1 1.23 us: local(): sums = jnp.sum(jnp.where(hit, every[:, topk:, None], 0.0), axis=(0, 1))]
  transfers between devices with their start and end apart: 1 -> 0, of which waited for: 0 -> 0; matrix products, arithmetic and copies ran while one was open for 0% -> 0% of each run, Pallas kernels for 0% -> 0%
where the time goes in v1:
time: 510 us
  Pallas kernels  420 us (82%)
  matrix products  34.2 us (7%)
  blocking collectives  34.1 us (7%)
  local copies, waits for them, and re-layouts  11.5 us (2%)
  other arithmetic  7.54 us (1%)
    pallas_call x1, Pallas kernels, local(): pl.pallas_call(functools.partial(return_kernel, nn, nl, nch), out_shape=j...  260 us
    pallas_call x1, Pallas kernels, local(): pl.pallas_call(functools.partial(dispatch_kernel, nn, nl, nch), out_shape...  160 us
    all_gather x1, blocking collectives, local(): every = lax.all_gather(both, ('node', 'local'), axis=0, tiled=True)  34.1 us
    dot_general x1, matrix products, local(): upper = jnp.dot(got, w_up[0], preferred_element_type=f32)  12.4 us
    dot_general x1, matrix products, local(): y = jnp.dot(hidden, w_down[0], preferred_element_type=f32).astype(bf16)  10.9 us
    dot_general x1, matrix products, local(): gate = jnp.dot(got, w_gate[0], preferred_element_type=f32)  10.8 us

profile of v1, /device:TPU:27, one launch (start us, length us, event | category | flops | bytes accessed | tf_op | source)
XLA Modules:
  0.0 509.9 jit_solution(7119488407503185180)
XLA Ops:
  0.6 0.7 convert_element_type.44
  1.3 0.7 pad_maximum_fusion.1
  2.0 34.1 %all_gather.3 = f32[4096,12]{0,1:T(8,128)S(1)} all-gather(f32[128,12]{0,1:T(8,128)S(1)} %pad_maximum_fusion.1), channel_id=1, replica_groups=mesh['node'=4,'local'=8] {'node','local'}, dimensions={0}, use_global_device_ids=true | all-gather | bytes 202752 | tf_op jit(solution)/shard_map/all_gather | solution.py:190
  36.2 0.1 copy.30
  36.3 0.1 compare_reduce_fusion
  36.4 0.2 bitcast_select_fusion.1
  36.7 0.1 iota_compare_fusion.2
  36.8 0.7 and_convert_fusion
  37.5 1.2 copy.33
  38.6 160.2 %shard_map.77 = bf16[8,128,5120]{2,1,0:T(8,128)(2,1)} custom-call(bf16[128,5120]{1,0:T(8,128)(2,1)} %tok.1, bf16[1024,512]{1,0:T(8,128)(2,1)} %bitcast.61), custom_call_target="tpu_custom_call" | custom-call | tf_op jit(solution)/shard_map/pallas_call | solution.py:224
  198.9 12.4 %fusion.1 = f32[1024,768]{1,0:T(8,128)S(1)} fusion(bf16[1024,5120]{1,0:T(8,128)(2,1)} %bitcast.59, bf16[1,5120,768]{2,1,0:T(8,128)(2,1)} %param.10), kind=kOutput, calls=%fused_computation.2 | convolution fusion | flops 8053063680 | bytes 21495808 | tf_op jit(solution)/shard_map/dot_general | solution.py:244
  211.3 10.8 %multiply_convert_fusion = bf16[1024,768]{1,0:T(8,128)(2,1)S(1)} fusion(f32[1024,768]{1,0:T(8,128)S(1)} %fusion.1, bf16[1024,5120]{1,0:T(8,128)(2,1)S(1)} %bitcast.60, bf16[1,5120,768]{2,1,0:T(8,128)(2,1)} %param.9), kind=kOutput, calls=%fused_computation.10 | convolution fusion | flops 8057782272 | bytes 23068672 | tf_op jit(solution)/shard_map/dot_general | solution.py:243
  222.1 10.9 %convolution_convert_fusion = bf16[1024,5120]{1,0:T(8,128)(2,1)} fusion(bf16[1024,768]{1,0:T(8,128)(2,1)S(1)} %multiply_convert_fusion, bf16[1,768,5120]{2,1,0:T(8,128)(2,1)S(1)} %bitcast.67), kind=kOutput, calls=%fused_computation | convolution fusion | flops 8058306560 | bytes 19922944 | tf_op jit(solution)/shard_map/dot_general | solution.py:246
  233.0 0.1 fusion.7
  233.1 0.1 copy.25
  233.2 0.1 iota_compare_fusion.1
  233.4 0.7 broadcast_and_fusion
  234.1 2.4 select_convert_fusion
  236.5 2.9 convert_element_type.54
  239.4 4.7 copy.28.mix
  244.2 259.6 %shard_map.78 = bf16[128,5120]{1,0:T(8,128)(2,1)} custom-call(bf16[8,128,5120]{2,1,0:T(8,128)(2,1)} %bitcast.58, bf16[1536,1024]{1,0:T(8,128)(2,1)} %copy.28.mix), custom_call_target="tpu_custom_call" | custom-call | tf_op jit(solution)/shard_map/pallas_call | solution.py:248
  503.8 1.2 select_reduce_fusion
  505.1 0.6 multiply_reduce_fusion
  506.3 2.5 copy.35
  (22 shorter events, 0.2 us)
Async XLA Ops:
  198.8 12.4 %copy-start = (bf16[8,128,5120]{2,1,0:T(8,128)(2,1)S(1)}, bf16[8,128,5120]{2,1,0:T(8,128)(2,1)}, u32[]{:S(2)}) copy-start(bf16[8,128,5120]{2,1,0:T(8,128)(2,1)} %shard_map.77) | copy-start | bytes 31457284
  198.9 23.2 %slice-start = ((s8[7864320]{0:T(1024)(128)(4,1)}), s8[4194304]{0:T(1024)(128)(4,1)S(1)}, s32[]{:S(2)}) async-start(s8[7864320]{0:T(1024)(128)(4,1)} %bitcast.66), calls=%async_computation | async-start | bytes 8388608
  211.3 10.8 %slice-start.1 = ((s8[7864320]{0:T(1024)(128)(4,1)}), s8[3670016]{0:T(1024)(128)(4,1)S(1)}, s32[]{:S(2)}) async-start(s8[7864320]{0:T(1024)(128)(4,1)} %bitcast.66), calls=%async_computation.1 | async-start | bytes 7340032

commit v2 on v1

--- a/solution.py
+++ b/solution.py
@@ -12,7 +12,7 @@
 
 
 def chunks_of(width):
-    return max(n for n in range(1, 9) if width % (n * 128) == 0)
+    return max(n for n in range(1, 11) if width % (n * 128) == 0)
 
 
 def greet(nn, nl, mn, ml):

time: 510 us -> 505 us (level)
  no operation moved by 1% of the time
where the time goes in v2:
time: 505 us; the launch traced here: 504 us
  Pallas kernels  415 us (82%)
  matrix products  34.2 us (7%)
  blocking collectives  34.1 us (7%)
  local copies, waits for them, and re-layouts  11.3 us (2%)
  other arithmetic  7.54 us (1%)
    pallas_call x1, Pallas kernels, local(): pl.pallas_call(functools.partial(return_kernel, nn, nl, nch), out_shape=j...  255 us
    pallas_call x1, Pallas kernels, local(): pl.pallas_call(functools.partial(dispatch_kernel, nn, nl, nch), out_shape...  160 us
    all_gather x1, blocking collectives, local(): every = lax.all_gather(both, ('node', 'local'), axis=0, tiled=True)  34.1 us
    dot_general x1, matrix products, local(): upper = jnp.dot(got, w_up[0], preferred_element_type=f32)  12.4 us
    dot_general x1, matrix products, local(): y = jnp.dot(hidden, w_down[0], preferred_element_type=f32).astype(bf16)  10.9 us
    dot_general x1, matrix products, local(): gate = jnp.dot(got, w_gate[0], preferred_element_type=f32)  10.8 us

profile of v2, /device:TPU:27, one launch (start us, length us, event | category | flops | bytes accessed | tf_op | source)
XLA Modules:
  0.0 504.4 jit_solution(16565919698793316753)
XLA Ops:
  0.6 0.7 convert_element_type.44
  1.3 0.7 pad_maximum_fusion.1
  2.0 34.1 %all_gather.3 = f32[4096,12]{0,1:T(8,128)S(1)} all-gather(f32[128,12]{0,1:T(8,128)S(1)} %pad_maximum_fusion.1), channel_id=1, replica_groups=mesh['node'=4,'local'=8] {'node','local'}, dimensions={0}, use_global_device_ids=true | all-gather | bytes 202752 | tf_op jit(solution)/shard_map/all_gather | solution.py:190
  36.2 0.1 copy.30
  36.3 0.1 compare_reduce_fusion
  36.4 0.2 bitcast_select_fusion.1
  36.7 0.1 iota_compare_fusion.2
  36.8 0.7 and_convert_fusion
  37.5 1.2 copy.33
  38.6 159.7 %shard_map.77 = bf16[8,128,5120]{2,1,0:T(8,128)(2,1)} custom-call(bf16[128,5120]{1,0:T(8,128)(2,1)} %tok.1, bf16[1024,512]{1,0:T(8,128)(2,1)} %bitcast.61), custom_call_target="tpu_custom_call" | custom-call | tf_op jit(solution)/shard_map/pallas_call | solution.py:224
  198.4 12.4 %fusion.1 = f32[1024,768]{1,0:T(8,128)S(1)} fusion(bf16[1024,5120]{1,0:T(8,128)(2,1)} %bitcast.59, bf16[1,5120,768]{2,1,0:T(8,128)(2,1)} %param.10), kind=kOutput, calls=%fused_computation.2 | convolution fusion | flops 8053063680 | bytes 21495808 | tf_op jit(solution)/shard_map/dot_general | solution.py:244
  210.8 10.8 %multiply_convert_fusion = bf16[1024,768]{1,0:T(8,128)(2,1)S(1)} fusion(f32[1024,768]{1,0:T(8,128)S(1)} %fusion.1, bf16[1024,5120]{1,0:T(8,128)(2,1)S(1)} %bitcast.60, bf16[1,5120,768]{2,1,0:T(8,128)(2,1)} %param.9), kind=kOutput, calls=%fused_computation.10 | convolution fusion | flops 8057782272 | bytes 23068672 | tf_op jit(solution)/shard_map/dot_general | solution.py:243
  221.6 10.9 %convolution_convert_fusion = bf16[1024,5120]{1,0:T(8,128)(2,1)} fusion(bf16[1024,768]{1,0:T(8,128)(2,1)S(1)} %multiply_convert_fusion, bf16[1,768,5120]{2,1,0:T(8,128)(2,1)S(1)} %bitcast.67), kind=kOutput, calls=%fused_computation | convolution fusion | flops 8058306560 | bytes 19922944 | tf_op jit(solution)/shard_map/dot_general | solution.py:246
  232.5 0.1 fusion.7
  232.6 0.1 copy.25
  232.7 0.1 iota_compare_fusion.1
  232.9 0.7 broadcast_and_fusion
  233.6 2.4 select_convert_fusion
  236.0 2.7 convert_element_type.54
  238.7 4.7 copy.28.mix
  243.5 254.8 %shard_map.78 = bf16[128,5120]{1,0:T(8,128)(2,1)} custom-call(bf16[8,128,5120]{2,1,0:T(8,128)(2,1)} %bitcast.58, bf16[1536,1024]{1,0:T(8,128)(2,1)} %copy.28.mix), custom_call_target="tpu_custom_call" | custom-call | tf_op jit(solution)/shard_map/pallas_call | solution.py:248
  498.3 1.2 select_reduce_fusion
  499.6 0.6 multiply_reduce_fusion
  500.8 2.5 copy.35
  (22 shorter events, 0.2 us)
Async XLA Ops:
  198.3 12.4 %copy-start = (bf16[8,128,5120]{2,1,0:T(8,128)(2,1)S(1)}, bf16[8,128,5120]{2,1,0:T(8,128)(2,1)}, u32[]{:S(2)}) copy-start(bf16[8,128,5120]{2,1,0:T(8,128)(2,1)} %shard_map.77) | copy-start | bytes 31457284
  198.3 23.2 %slice-start = ((s8[7864320]{0:T(1024)(128)(4,1)}), s8[4194304]{0:T(1024)(128)(4,1)S(1)}, s32[]{:S(2)}) async-start(s8[7864320]{0:T(1024)(128)(4,1)} %bitcast.66), calls=%async_computation | async-start | bytes 8388608
  210.8 10.8 %slice-start.1 = ((s8[7864320]{0:T(1024)(128)(4,1)}), s8[3670016]{0:T(1024)(128)(4,1)S(1)}, s32[]{:S(2)}) async-start(s8[7864320]{0:T(1024)(128)(4,1)} %bitcast.66), calls=%async_computation.1 | async-start | bytes 7340032
